TPU v7x, 32 devices: a whole 2x2x4 slice. The times are simulated.
32 devices in a mesh: dp: 8 (over z, x), expert: 4 (over y, core).
Axes of the slice: x: 2, y: 2, z: 4, core: 2. Of those that a mesh axis runs over, the one named last changes fastest.
Arguments:
- tokens: bfloat16 [2, 8192, 1024], P(None, ('dp', 'expert')), may hold values from -6 to 6
- lengths: int32 [2, 8], P(None, 'dp'), may hold values from 256 to 1024, as said below
- routes: int32 [2, 8192, 2], P(None, ('dp', 'expert')), may hold values from 0 to 3, all different within a row
- w_qkv: bfloat16 [1024, 3072], P(('dp', 'expert')), may hold values from -0.1875 to 0.1875
- w_out: bfloat16 [1024, 1024], P(('dp', 'expert')), may hold values from -3 to 3
- norm_gains: bfloat16 [1024, 2], P(('dp', 'expert')), may hold values from 0.5 to 1.5
- bias_table: bfloat16 [512], P(('dp', 'expert')), may hold values from -4 to 4
- router: bfloat16 [1024, 4], P(('dp', 'expert')), may hold values from -0.09375 to 0.09375
- w_in: bfloat16 [4, 1024, 5632], P('expert', 'dp'), may hold values from -0.1875 to 0.1875
- w_down: bfloat16 [4, 2816, 1024], P('expert', 'dp'), may hold values from -0.4375 to 0.4375
- cotangent: bfloat16 [2, 8192, 1024], P(None, ('dp', 'expert')), may hold values from -6 to 6
Outputs:
- block_out: bfloat16 [2, 8192, 1024], P(None, ('dp', 'expert'))
- grad_tokens: float32 [2, 8192, 1024], P(None, ('dp', 'expert'))
- grad_qkv: float32 [1024, 3072], P(('dp', 'expert'))
- grad_out_proj: float32 [1024, 1024], P(('dp', 'expert'))
- grad_gains: float32 [1024, 2], P(('dp', 'expert'))
- grad_bias: float32 [512], P(('dp', 'expert'))
- grad_router: float32 [1024, 4], P(('dp', 'expert'))
- grad_w_in: float32 [4, 1024, 5632], P('expert', 'dp')
- grad_w_down: float32 [4, 2816, 1024], P('expert', 'dp')
Inputs may be any that keep to these rules, and one draw needn't show every extreme that they name: `lengths`: each sequence has at least 256 live tokens; some sequence is exactly 1024 long.
All inputs are finite; a program needn't handle non-finite values.
Results may differ from a plain program's by a relative error of at most 0.02.
Values may be sent and summed in bfloat16 or wider, within the bound.
A program may use at most 320 MiB of HBM per device.

v0:
```python
import jax
import jax.numpy as jnp
from jax import lax
from jax.sharding import PartitionSpec as P

D = 1024
H = 16
DH = 64
FF = 2816
BUCKETS = 32
TOP = 2
bucket_edges = (12, 16, 23, 32, 46, 64, 91)
norm_eps = 1e-06
highest = lax.Precision.HIGHEST


def bucket_ids(query_pos, key_pos):
    offset = key_pos[None, :] - query_pos[:, None]
    dist = jnp.abs(offset)
    beyond = jnp.zeros_like(dist)
    for edge in bucket_edges:
        beyond = beyond + (dist >= edge).astype(jnp.int32)
    near = jnp.where(dist < 8, dist, 8 + beyond)
    return near + 16 * (offset > 0).astype(jnp.int32)


def rms_scale(values, gain):
    return values * lax.rsqrt(jnp.mean(values * values, axis=-1, keepdims=True) + norm_eps) * gain


def geglu(joined):
    half = joined.shape[-1] // 2
    return jax.nn.gelu(joined[..., :half], approximate=True) * joined[..., half:]


def slot_tables(route_rows, live, experts, capacity):
    count, top = route_rows.shape
    picks = (route_rows[:, :, None] == jnp.arange(experts, dtype=jnp.int32)[None, None, :]).astype(
        jnp.int32
    ) * live[:, None, None]
    flat = picks.reshape(count * top, experts)
    before = jnp.cumsum(flat, axis=0) - flat
    place = jnp.sum(before * flat, axis=1).reshape(count, top)
    kept = (place < capacity) & (live[:, None] > 0)
    target = jnp.where(kept, route_rows * capacity + place, -1)
    columns = jnp.arange(experts * capacity, dtype=jnp.int32)
    return target[:, :, None] == columns[None, None, :]


def matmul(left, right):
    return jnp.dot(left, right, preferred_element_type=jnp.float32)


def inner_rows(left, right):
    return jnp.einsum("ti,tj->ij", left, right, preferred_element_type=jnp.float32)


def times_trans(left, right):
    return jnp.einsum("ti,ji->tj", left, right, preferred_element_type=jnp.float32)


def local(
    tokens, lengths, routes, w_qkv, w_out, norm_gains, bias_table, router, w_in, w_down, cotangent
):
    micro, rows, width = tokens.shape
    experts = lax.axis_size("expert")
    seq_len = rows * experts
    capacity = (5 * rows * TOP + 4 * experts - 1) // (4 * experts)
    scale = DH ** (-0.5)
    query_pos = lax.axis_index("expert") * rows + jnp.arange(rows, dtype=jnp.int32)
    key_pos = jnp.arange(seq_len, dtype=jnp.int32)
    bucket_hot = (
        bucket_ids(query_pos, key_pos)[:, :, None]
        == jnp.arange(BUCKETS, dtype=jnp.int32)[None, None, :]
    ).astype(jnp.float32)
    expert_hot = jnp.arange(experts, dtype=jnp.int32)
    acc_qkv = jnp.zeros((D, 3 * D), jnp.float32)
    acc_out = jnp.zeros((D, D), jnp.float32)
    acc_gains = jnp.zeros((D, 2), jnp.float32)
    acc_bias = jnp.zeros((BUCKETS, H), jnp.float32)
    acc_router = jnp.zeros((D, experts), jnp.float32)
    acc_in = jnp.zeros((D, 2 * FF), jnp.float32)
    acc_down = jnp.zeros((FF, D), jnp.float32)
    outputs = []
    input_grads = []
    for step in range(micro):
        (wqkv, wout, gains, table_flat, route_w), (win, wdown) = (
            (
                lax.all_gather(w_qkv, ("dp", "expert"), axis=0, tiled=True),
                lax.all_gather(w_out, ("dp", "expert"), axis=0, tiled=True),
                lax.all_gather(norm_gains, ("dp", "expert"), axis=0, tiled=True),
                lax.all_gather(bias_table, ("dp", "expert"), axis=0, tiled=True),
                lax.all_gather(router, ("dp", "expert"), axis=0, tiled=True),
            ),
            (
                lax.all_gather(w_in, "dp", axis=1, tiled=True),
                lax.all_gather(w_down, "dp", axis=1, tiled=True),
            ),
        )
        gains_f = gains.astype(jnp.float32)
        table = table_flat.astype(jnp.float32).reshape(BUCKETS, H)
        x_rows = tokens[step].astype(jnp.float32)
        length = lengths[step, 0]
        key_live = key_pos < length
        h1 = rms_scale(x_rows, gains_f[:, 0]).astype(jnp.bfloat16)
        qkv = matmul(h1, wqkv)
        query = qkv[:, :D].astype(jnp.bfloat16)
        keys_low = qkv[:, D : 2 * D].astype(jnp.bfloat16)
        values_low = qkv[:, 2 * D :].astype(jnp.bfloat16)
        keys_all, values_all = (
            lax.all_gather(keys_low, "expert", axis=0, tiled=True),
            lax.all_gather(values_low, "expert", axis=0, tiled=True),
        )
        query_heads = query.reshape(rows, H, DH)
        key_heads = keys_all.reshape(seq_len, H, DH)
        value_heads = values_all.reshape(seq_len, H, DH)
        bias = jnp.einsum("qkb,bh->hqk", bucket_hot, table, precision=highest)
        scores = (
            scale
            * jnp.einsum("qhd,khd->hqk", query_heads, key_heads, preferred_element_type=jnp.float32)
            + bias
        )
        scores = jnp.where(key_live[None, None, :], scores, -1e30)
        top_score = jnp.max(scores, axis=-1, keepdims=True)
        lse = top_score + jnp.log(jnp.sum(jnp.exp(scores - top_score), axis=-1, keepdims=True))
        probs = jnp.exp(scores - lse)
        probs_low = probs.astype(jnp.bfloat16)
        attended = jnp.einsum(
            "hqk,khd->qhd", probs_low, value_heads, preferred_element_type=jnp.float32
        )
        attended_low = attended.astype(jnp.bfloat16)
        attended_low = attended_low.reshape(rows, D)
        x_mid = x_rows + matmul(attended_low, wout)
        h2 = rms_scale(x_mid, gains_f[:, 1]).astype(jnp.bfloat16)
        logits = matmul(h2, route_w)
        route_probs = jax.nn.softmax(logits, axis=-1)
        chosen = routes[step]
        route_hot = (chosen[:, :, None] == expert_hot[None, None, :]).astype(jnp.float32)
        gates = jnp.sum(route_probs[:, None, :] * route_hot, axis=-1)
        live = (query_pos < length).astype(jnp.int32)
        slot_hot = slot_tables(chosen, live, experts, capacity)
        slot_low = slot_hot.astype(jnp.bfloat16)
        any_slot = jnp.sum(slot_low, axis=1)
        sent = jnp.einsum("ts,td->sd", any_slot, h2, preferred_element_type=jnp.float32).astype(
            jnp.bfloat16
        )
        arrived = lax.all_to_all(
            sent.reshape(experts, capacity, D), "expert", split_axis=0, concat_axis=0, tiled=True
        )
        arrived_rows = arrived.reshape(experts * capacity, D)
        joined = matmul(arrived_rows, win[0])
        acted = geglu(joined).astype(jnp.bfloat16)
        produced = matmul(acted, wdown[0]).astype(jnp.bfloat16)
        returned = lax.all_to_all(
            produced.reshape(experts, capacity, D),
            "expert",
            split_axis=0,
            concat_axis=0,
            tiled=True,
        )
        returned_rows = returned.reshape(experts * capacity, D)
        picked = jnp.einsum(
            "tks,sd->tkd", slot_low, returned_rows, preferred_element_type=jnp.float32
        )
        mixed = jnp.sum(gates[:, :, None] * picked, axis=1)
        outputs.append((x_mid + mixed).astype(jnp.bfloat16))
        grad_out = cotangent[step].astype(jnp.float32)
        grad_gates = jnp.sum(grad_out[:, None, :] * picked, axis=-1)
        weighted = gates[:, :, None] * grad_out[:, None, :]
        grad_returned = jnp.einsum(
            "tks,tkd->sd", slot_hot.astype(jnp.float32), weighted, precision=highest
        ).astype(jnp.bfloat16)
        grad_produced = lax.all_to_all(
            grad_returned.reshape(experts, capacity, D),
            "expert",
            split_axis=0,
            concat_axis=0,
            tiled=True,
        )
        grad_produced = grad_produced.reshape(experts * capacity, D)
        acc_down = acc_down + inner_rows(acted, grad_produced)
        grad_acted = times_trans(grad_produced, wdown[0])
        geglu_pull = jax.vjp(geglu, joined)[1]
        grad_joined = geglu_pull(grad_acted)[0].astype(jnp.bfloat16)
        acc_in = acc_in + inner_rows(arrived_rows, grad_joined)
        grad_arrived = times_trans(grad_joined, win[0]).astype(jnp.bfloat16)
        grad_sent = lax.all_to_all(
            grad_arrived.reshape(experts, capacity, D),
            "expert",
            split_axis=0,
            concat_axis=0,
            tiled=True,
        )
        grad_h2 = jnp.einsum(
            "ts,sd->td",
            any_slot,
            grad_sent.reshape(experts * capacity, D),
            preferred_element_type=jnp.float32,
        )
        grad_route = jnp.sum(grad_gates[:, :, None] * route_hot, axis=1)
        grad_logits = route_probs * (
            grad_route - jnp.sum(route_probs * grad_route, axis=-1, keepdims=True)
        )
        grad_logits = grad_logits.astype(jnp.bfloat16)
        acc_router = acc_router + inner_rows(h2, grad_logits)
        grad_h2 = grad_h2 + times_trans(grad_logits, route_w)
        norm_pull = jax.vjp(rms_scale, x_mid, gains_f[:, 1])[1]
        grad_mid, grad_gain_two = norm_pull(grad_h2)
        grad_mid = grad_mid + grad_out
        grad_mid_low = grad_mid.astype(jnp.bfloat16)
        acc_out = acc_out + inner_rows(attended_low, grad_mid_low)
        grad_attended = times_trans(grad_mid_low, wout).astype(jnp.bfloat16).reshape(rows, H, DH)
        again = (
            scale
            * jnp.einsum("qhd,khd->hqk", query_heads, key_heads, preferred_element_type=jnp.float32)
            + bias
        )
        again = jnp.where(key_live[None, None, :], again, -1e30)
        probs_again = jnp.exp(again - lse)
        grad_values = jnp.einsum(
            "hqk,qhd->khd",
            probs_again.astype(jnp.bfloat16),
            grad_attended,
            preferred_element_type=jnp.float32,
        )
        grad_probs = jnp.einsum(
            "qhd,khd->hqk", grad_attended, value_heads, preferred_element_type=jnp.float32
        )
        weight_sum = jnp.sum(probs_again * grad_probs, axis=-1, keepdims=True)
        grad_scores = (probs_again * (grad_probs - weight_sum)).astype(jnp.bfloat16)
        grad_query = (
            scale
            * jnp.einsum("hqk,khd->qhd", grad_scores, key_heads, preferred_element_type=jnp.float32)
        ).astype(jnp.bfloat16)
        grad_keys = scale * jnp.einsum(
            "hqk,qhd->khd", grad_scores, query_heads, preferred_element_type=jnp.float32
        )
        acc_bias = acc_bias + jnp.einsum(
            "hqk,qkb->bh", grad_scores.astype(jnp.float32), bucket_hot, precision=highest
        )
        key_grads, value_grads = (
            lax.psum_scatter(
                grad_keys.reshape(seq_len, D).astype(jnp.bfloat16),
                "expert",
                scatter_dimension=0,
                tiled=True,
            ).astype(jnp.float32),
            lax.psum_scatter(
                grad_values.reshape(seq_len, D).astype(jnp.bfloat16),
                "expert",
                scatter_dimension=0,
                tiled=True,
            ).astype(jnp.float32),
        )
        grad_qkv = jnp.concatenate(
            [
                grad_query.reshape(rows, D),
                key_grads.astype(jnp.bfloat16),
                value_grads.astype(jnp.bfloat16),
            ],
            axis=1,
        )
        acc_qkv = acc_qkv + inner_rows(h1, grad_qkv)
        grad_h1 = times_trans(grad_qkv, wqkv)
        first_pull = jax.vjp(rms_scale, x_rows, gains_f[:, 0])[1]
        grad_x, grad_gain_one = first_pull(grad_h1)
        acc_gains = acc_gains + jnp.stack([grad_gain_one, grad_gain_two], axis=1)
        input_grads.append(grad_x + grad_mid)
    block_parts = (
        lax.psum_scatter(acc_qkv, ("dp", "expert"), scatter_dimension=0, tiled=True),
        lax.psum_scatter(acc_out, ("dp", "expert"), scatter_dimension=0, tiled=True),
        lax.psum_scatter(acc_gains, ("dp", "expert"), scatter_dimension=0, tiled=True),
        lax.psum_scatter(
            acc_bias.reshape(BUCKETS * H), ("dp", "expert"), scatter_dimension=0, tiled=True
        ),
        lax.psum_scatter(acc_router, ("dp", "expert"), scatter_dimension=0, tiled=True),
    )
    expert_parts = (
        lax.psum_scatter(
            acc_in[None].astype(jnp.bfloat16), "dp", scatter_dimension=1, tiled=True
        ).astype(jnp.float32),
        lax.psum_scatter(
            acc_down[None].astype(jnp.bfloat16), "dp", scatter_dimension=1, tiled=True
        ).astype(jnp.float32),
    )
    return (
        jnp.stack(outputs, axis=0),
        jnp.stack(input_grads, axis=0),
        block_parts[0],
        block_parts[1],
        block_parts[2],
        block_parts[3],
        block_parts[4],
        expert_parts[0],
        expert_parts[1],
    )


def solution(mesh):
    in_specs = (
        P(None, ("dp", "expert"), None),
        P(None, "dp"),
        P(None, ("dp", "expert"), None),
        P(("dp", "expert"), None),
        P(("dp", "expert"), None),
        P(("dp", "expert"), None),
        P(("dp", "expert")),
        P(("dp", "expert"), None),
        P("expert", "dp", None),
        P("expert", "dp", None),
        P(None, ("dp", "expert"), None),
    )
    out_specs = (
        P(None, ("dp", "expert"), None),
        P(None, ("dp", "expert"), None),
        P(("dp", "expert"), None),
        P(("dp", "expert"), None),
        P(("dp", "expert"), None),
        P(("dp", "expert")),
        P(("dp", "expert"), None),
        P("expert", "dp", None),
        P("expert", "dp", None),
    )
    return jax.shard_map(local, mesh=mesh, in_specs=in_specs, out_specs=out_specs, check_vma=False)
```

profile of v0, /device:TPU:0, one launch (start us, length us, event | category | flops | bytes accessed | tf_op | source)
XLA Modules:
  0.0 1743.3 jit_solution(17928922391032202754)
XLA Ops:
  8.0 43.5 %all-gather = bf16[32,32,2]{1,2,0:T(2,128)(2,1)S(1)} all-gather(bf16[1,32,2]{1,2,0:T(2,128)(2,1)} %bitcast.309), channel_id=1, replica_groups=mesh['dp'=8,'expert'=4] {'dp','expert'}, dimensions={0}, use_global_device_ids=true | all-gather | bytes 4224 | tf_op jit(solution)/shard_map/all_gather | solution.py:91
  53.1 29.9 %all-gather.11.cloned.1.call-done = bf16[1024,3072]{1,0:T(8,128)(2,1)} async-done(((bf16[32,3072]{1,0:T(8,128)(2,1)}), bf16[1024,3072]{1,0:T(8,128)(2,1)}) %all-gather.11.cloned.1.call-update) | async-done | bytes 6291472 | tf_op jit(solution)/shard_map/all_gather | solution.py:89
  82.9 4.9 convolution_convert_fusion.1
  90.5 4.7 convolution_convert_fusion
  106.2 7.9 iota_compare_fusion
  114.2 46.5 %copy.135 = pred[256,1024,32]{1,2,0:T(32,128)(4,1)} copy(pred[256,1024,32]{0,2,1:T(32,128)(4,1)} %iota_compare_fusion) | data formatting | bytes 16777216 | tf_op jit(solution)/shard_map/eq | solution.py:73
  161.0 39.7 %all-reduce.4 = bf16[512]{0:T(512)(128)(2,1)S(1)} all-reduce(bf16[512]{0:T(512)(128)(2,1)S(1)} %dynamic-update-slice), channel_id=1, replica_groups=mesh['dp'=8,'expert'=4] {'dp','expert'}, use_global_device_ids=true, to_apply=%add.4 | all-reduce | flops 512 | bytes 2048
  204.2 40.5 %all-gather.1 = bf16[32,32,4]{1,2,0:T(4,128)(2,1)S(1)} all-gather(bf16[1,32,4]{1,2,0:T(4,128)(2,1)S(1)} %bitcast.308), channel_id=1, replica_groups=mesh['dp'=8,'expert'=4] {'dp','expert'}, dimensions={0}, use_global_device_ids=true | all-gather | bytes 8448 | tf_op jit(solution)/shard_map/all_gather | solution.py:93
  247.5 10.6 fusion.142
  269.6 22.4 %fusion.171 = (f32[16,256]{1,0:T(8,128)S(1)}, f32[16,256,1024]{2,1,0:T(8,128)}) fusion(f32[16,256,1024]{2,0,1:T(8,128)} %fusion.142, bf16[256,16,64]{0,2,1:T(8,128)(2,1)} %bitcast.260, bf16[1024,16,64]{0,2,1:T(8,128)(2,1)S(1)} %bitcast.250, pred[1024]{0:T(1024)(128)(4,1)S(1)} %iota_compare_fusion.22), kind=kOutput, calls=%fused_computation.267 | convolution fusion | flops 553644032 | bytes 36193280 | tf_op jit(solution)/shard_map/qhd,khd->hqk/dot_general | solution.py:120
  292.0 7.8 exponential_reduce_fusion.1
  299.9 8.6 fusion.76
  315.1 4.8 all-to-all-start
  322.8 22.4 %fusion.173 = (f32[16,256]{1,0:T(8,128)S(1)}, f32[16,256,1024]{2,1,0:T(8,128)}) fusion(f32[16,256,1024]{2,0,1:T(8,128)} %fusion.142, bf16[256,16,64]{0,2,1:T(8,128)(2,1)} %bitcast.262, bf16[1024,16,64]{0,2,1:T(8,128)(2,1)S(1)} %bitcast.252, pred[1024]{0:T(1024)(128)(4,1)S(1)} %iota_compare_fusion.21), kind=kOutput, calls=%fused_computation.269 | convolution fusion | flops 553644032 | bytes 36193280 | tf_op jit(solution)/shard_map/qhd,khd->hqk/dot_general | solution.py:120
  345.3 7.8 exponential_reduce_fusion
  365.0 42.5 %all-gather.19.cloned.1.call-done = bf16[1,1024,5632]{2,1,0:T(8,128)(2,1)} async-done(((bf16[1,128,5632]{2,1,0:T(8,128)(2,1)}), bf16[1,1024,5632]{2,1,0:T(8,128)(2,1)}) %all-gather.19.cloned.1.call-update) | async-done | bytes 11534352 | tf_op jit(solution)/shard_map/all_gather | solution.py:96
  407.5 13.7 fusion.12
  421.2 79.0 %all-gather.21.cloned.1.call-done = bf16[1,2816,1024]{2,1,0:T(8,128)(2,1)} async-done(((bf16[1,352,1024]{2,1,0:T(8,128)(2,1)}), bf16[1,2816,1024]{2,1,0:T(8,128)(2,1)}) %all-gather.21.cloned.1.call-update) | async-done | bytes 5767184 | tf_op jit(solution)/shard_map/all_gather | solution.py:97
  500.2 18.8 %fusion.36 = (f32[640,2816]{1,0:T(8,128)}, f32[640,2816]{1,0:T(8,128)}, bf16[640,2816]{1,0:T(8,128)(2,1)}) fusion(f32[640,5632]{1,0:T(8,128)} %fusion.12, bf16[640,1024]{1,0:T(8,128)(2,1)S(1)} %bitcast.282, bf16[1,2816,1024]{2,1,0:T(8,128)(2,1)} %all-gather.21.cloned.1.call-done), kind=kOutput, calls=%fused_computation.67 | convolution fusion | flops 3734241280 | bytes 39518208 | tf_op jit(solution)/shard_map/ti,ji->tj/dot_general | solution.py:59
  519.1 15.5 fusion.66
  538.1 8.7 fusion.60
  546.8 8.5 all-to-all-done.5
  555.3 4.5 all-to-all-start.1
  559.9 9.3 fusion.79
  572.5 4.6 all-to-all-done.1
  587.1 4.3 all-to-all-start.2
  592.9 4.9 bitcast_convert_fusion
  597.8 10.9 all-to-all-done.2
  608.7 4.7 all-to-all-start.6
  613.4 13.8 fusion.10
  630.7 17.9 %fusion.37 = (f32[640,2816]{1,0:T(8,128)}, f32[640,2816]{1,0:T(8,128)}, bf16[640,2816]{1,0:T(8,128)(2,1)}) fusion(f32[640,5632]{1,0:T(8,128)} %fusion.10, bf16[640,1024]{1,0:T(8,128)(2,1)} %bitcast.58, bf16[1,2816,1024]{2,1,0:T(8,128)(2,1)} %all-gather.21.cloned.1.call-done), kind=kOutput, calls=%fused_computation.68 | convolution fusion | flops 3734241280 | bytes 39518208 | tf_op jit(solution)/shard_map/ti,ji->tj/dot_general | solution.py:59
  648.6 15.5 fusion.69
  664.0 4.5 all-to-all-start.7
  668.5 8.7 fusion.63
  677.3 8.5 all-to-all-done.7
  685.8 4.3 all-to-all-start.3
  693.1 14.3 all-to-all-done.3
  716.9 9.1 fusion.53
  726.0 9.9 multiply_reduce_fusion
  735.9 8.0 multiply_convert_fusion
  751.7 9.3 fusion.50
  761.1 10.7 multiply_reduce_fusion.1
  771.7 8.1 multiply_convert_fusion.1
  784.3 9.6 fusion.178
  795.4 8.4 fusion.83
  803.8 6.9 fusion.82
  810.9 6.2 fusion.126
  817.0 5.4 reduce-scatter.17.cloned.1.call-done
  822.5 34.2 %reduce-scatter.15.cloned.1.call-done = bf16[256,1024]{0,1:T(8,128)(2,1)} async-done(((bf16[1024,1024]{0,1:T(8,128)(2,1)}), bf16[256,1024]{0,1:T(8,128)(2,1)}) %reduce-scatter.15.cloned.1.call-update) | async-done | bytes 524304 | tf_op jit(solution)/shard_map/reduce_scatter | solution.py:242
  856.7 6.3 fusion.94
  864.2 13.0 fusion.35
  877.3 19.1 %fusion.119 = f32[1024,5632]{1,0:T(8,128)} fusion(bf16[640,1024]{1,0:T(8,128)(2,1)} %bitcast.17, f32[640,2816]{1,0:T(8,128)} %get-tuple-element.26, f32[640,2816]{1,0:T(8,128)} %get-tuple-element.25), kind=kOutput, calls=%fused_computation.171 | convolution fusion | flops 7389184000 | bytes 38797312 | tf_op jit(solution)/shard_map/ti,tj->ij/dot_general | solution.py:55
  896.4 21.3 %fusion.14 = bf16[1,1024,5632]{2,1,0:T(8,128)(2,1)} fusion(f32[1024,5632]{1,0:T(8,128)} %fusion.119, bf16[640,1024]{1,0:T(8,128)(2,1)} %bitcast.36, f32[640,2816]{1,0:T(8,128)} %get-tuple-element.28, f32[640,2816]{1,0:T(8,128)} %get-tuple-element.27), kind=kOutput, calls=%fused_computation.33 | convolution fusion | flops 7400718336 | bytes 50331648 | tf_op jit(solution)/shard_map/ti,tj->ij/dot_general | solution.py:55
  927.3 6.6 convolution_add_fusion
  933.9 12.7 copy.156
  946.6 12.6 copy.157
  959.2 7.6 fusion.88
  966.9 5.3 fusion.90
  972.3 39.4 %all-reduce.5 = f32[512]{0:T(512)S(1)} all-reduce(f32[512]{0:T(512)S(1)} %reshape.487), channel_id=9, replica_groups=mesh['dp'=8,'expert'=4] {'dp','expert'}, use_global_device_ids=true, to_apply=%region_47.48.clone | all-reduce | flops 512 | bytes 4096
  1019.6 109.5 %reduce-scatter.31.cloned.1.call-done = f32[32,2]{1,0:T(8,128)} async-done(((f32[1024,2]{1,0:T(8,128)}), f32[32,2]{1,0:T(8,128)}) %reduce-scatter.31.cloned.1.call-update) | async-done | bytes 272
  1130.5 108.7 %reduce-scatter.29.cloned.1.call-done = bf16[1,352,1024]{2,1,0:T(8,128)(2,1)} async-done(((bf16[1,2816,1024]{2,1,0:T(8,128)(2,1)}), bf16[1,352,1024]{2,1,0:T(8,128)(2,1)}) %reduce-scatter.29.cloned.1.call-update) | async-done | bytes 720912 | tf_op jit(solution)/shard_map/reduce_scatter | solution.py:282
  1241.6 193.3 %reduce-scatter.27.cloned.1.call-done = bf16[1,128,5632]{2,1,0:T(8,128)(2,1)} async-done(((bf16[1,1024,5632]{2,1,0:T(8,128)(2,1)}), bf16[1,128,5632]{2,1,0:T(8,128)(2,1)}) %reduce-scatter.27.cloned.1.call-update) | async-done | bytes 1441808 | tf_op jit(solution)/shard_map/reduce_scatter | solution.py:279
  1438.1 140.8 %reduce-scatter.25.cloned.1.call-done = f32[32,1024]{1,0:T(8,128)} async-done(((f32[1024,1024]{1,0:T(8,128)}), f32[32,1024]{1,0:T(8,128)}) %reduce-scatter.25.cloned.1.call-update) | async-done | bytes 131088 | tf_op jit(solution)/shard_map/reduce_scatter | solution.py:271
  1578.9 157.2 %reduce-scatter.23.cloned.1.call-done = f32[32,3072]{1,0:T(8,128)} async-done(((f32[1024,3072]{1,0:T(8,128)}), f32[32,3072]{1,0:T(8,128)}) %reduce-scatter.23.cloned.1.call-update) | async-done | bytes 393232 | tf_op jit(solution)/shard_map/reduce_scatter | solution.py:270
  (341 shorter events, 129.0 us)
Async XLA Ops:
  7.2 75.8 %all-gather.11.cloned.1.call-start = ((), (), s32[]{:S(2)}) async-start(), calls=%async_computation.18 | async-start | bytes 6488064 | tf_op jit(solution)/shard_map/all_gather | solution.py:89
  7.9 254.9 %all-gather.13.cloned.1.call-start = ((), (), s32[]{:S(2)}) async-start(), calls=%async_computation.19 | async-start | bytes 2621440 | tf_op jit(solution)/shard_map/all_gather | solution.py:112
  53.0 34.9 %copy-start.75 = (f32[256]{0:T(256)}, f32[256]{0:T(256)S(1)}, u32[]{:S(2)}) copy-start(f32[256]{0:T(256)S(1)} %get-tuple-element.23) | copy-start | bytes 3076
  53.0 37.4 %copy-start.77 = (f32[256]{0:T(256)}, f32[256]{0:T(256)S(1)}, u32[]{:S(2)}) copy-start(f32[256]{0:T(256)S(1)} %get-tuple-element.24) | copy-start | bytes 3076
  53.0 34.8 %copy-start.59 = (f32[256]{0:T(256)}, f32[256]{0:T(256)S(1)}, u32[]{:S(2)}) copy-start(f32[256]{0:T(256)S(1)} %fusion.154) | copy-start | bytes 3076
  53.1 37.4 %copy-start.45 = (f32[1024,1]{0,1:T(1,128)}, f32[1024,1]{0,1:T(1,128)S(1)}, u32[]{:S(2)}) copy-start(f32[1024,1]{0,1:T(1,128)S(1)} %get-tuple-element.46) | copy-start | bytes 12292
  89.0 177.7 %all-gather.15.cloned.1.call-start = ((), (), s32[]{:S(2)}) async-start(), calls=%async_computation.20 | async-start | bytes 2621440 | tf_op jit(solution)/shard_map/all_gather | solution.py:111
  89.8 218.7 %all-gather.17.cloned.1.call-start = ((), (), s32[]{:S(2)}) async-start(), calls=%async_computation.21 | async-start | bytes 2162688 | tf_op jit(solution)/shard_map/all_gather | solution.py:90
  90.3 229.6 %all-gather.25.cloned.1.call-start = ((), (), s32[]{:S(2)}) async-start(), calls=%async_computation.25 | async-start | bytes 2621440 | tf_op jit(solution)/shard_map/all_gather | solution.py:111
  90.4 10.6 copy-start.79
  96.3 257.1 %all-gather.23.cloned.1.call-start = ((), (), s32[]{:S(2)}) async-start(), calls=%async_computation.24 | async-start | bytes 2621440 | tf_op jit(solution)/shard_map/all_gather | solution.py:112
  96.9 310.6 %all-gather.19.cloned.1.call-start = ((), (), s32[]{:S(2)}) async-start(), calls=%async_computation.22 | async-start | bytes 12976128 | tf_op jit(solution)/shard_map/all_gather | solution.py:96
  97.7 402.6 %all-gather.21.cloned.1.call-start = ((), (), s32[]{:S(2)}) async-start(), calls=%async_computation.23 | async-start | bytes 6488064 | tf_op jit(solution)/shard_map/all_gather | solution.py:97
  106.2 54.5 %copy-start.32 = (s32[256,1024]{0,1:T(8,128)}, s32[256,1024]{0,1:T(8,128)S(1)}, u32[]{:S(2)}) copy-start(s32[256,1024]{0,1:T(8,128)S(1)} %fusion.105) | copy-start | bytes 3145732
  114.2 46.5 %copy-start.82 = (bf16[16]{0:T(256)(128)(2,1)S(1)}, bf16[16]{0:T(256)(128)(2,1)}, u32[]{:S(2)}) copy-start(bf16[16]{0:T(256)(128)(2,1)} %param.17) | copy-start | bytes 100
  114.2 90.0 %copy-start.81 = (bf16[32,4]{0,1:T(4,128)(2,1)S(1)}, bf16[32,4]{0,1:T(4,128)(2,1)}, u32[]{:S(2)}) copy-start(bf16[32,4]{0,1:T(4,128)(2,1)} %param.18) | copy-start | bytes 772
  247.5 11.6 copy-start.29
  247.5 14.2 copy-start.39
  269.6 22.4 %copy-start.4 = (bf16[1024,1024]{0,1:T(8,128)(2,1)}, bf16[1024,1024]{0,1:T(8,128)(2,1)S(1)}, u32[]{:S(2)}) copy-start(bf16[1024,1024]{0,1:T(8,128)(2,1)S(1)} %copy.133) | copy-start | bytes 6291460
  299.8 13.7 copy-start.36
  308.4 11.5 copy-start.28
  311.6 33.6 %copy-start.73 = (f32[256]{0:T(256)}, f32[256]{0:T(256)S(1)}, u32[]{:S(2)}) copy-start(f32[256]{0:T(256)S(1)} %get-tuple-element.54) | copy-start | bytes 3076
  315.1 46.1 %all-to-all-start = ((bf16[4,160,1024]{2,1,0:T(8,128)(2,1)}), bf16[4,160,1024]{2,1,0:T(8,128)(2,1)}, u32[]{:S(2)}, u32[]{:S(2)}) async-start(bf16[4,160,1024]{2,1,0:T(8,128)(2,1)} %bitcast.16), calls=%async_computation | async-start | bytes 2621440 | tf_op jit(solution)/shard_map/all_to_all | solution.py:147
  322.8 22.5 %copy-start.6 = (bf16[1024,1024]{0,1:T(8,128)(2,1)}, bf16[1024,1024]{0,1:T(8,128)(2,1)S(1)}, u32[]{:S(2)}) copy-start(bf16[1024,1024]{0,1:T(8,128)(2,1)S(1)} %copy.146) | copy-start | bytes 6291460
  345.3 12.2 copy-start.43
  353.4 227.6 %copy-start.53 = (f32[256,4]{0,1:T(4,128)}, f32[256,4]{0,1:T(4,128)S(1)}, u32[]{:S(2)}) copy-start(f32[256,4]{0,1:T(4,128)S(1)} %get-tuple-element.57) | copy-start | bytes 12292
  353.4 227.6 %copy-start.57 = (f32[256]{0:T(256)}, f32[256]{0:T(256)S(1)}, u32[]{:S(2)}) copy-start(f32[256]{0:T(256)S(1)} %get-tuple-element.56) | copy-start | bytes 3076
  357.4 223.6 %copy-start.61 = (f32[256]{0:T(256)}, f32[256]{0:T(256)S(1)}, u32[]{:S(2)}) copy-start(f32[256]{0:T(256)S(1)} %fusion.147) | copy-start | bytes 3076
  357.5 202.4 %copy-start.51 = (f32[16,256]{1,0:T(8,128)}, f32[16,256]{1,0:T(8,128)S(1)}, u32[]{:S(2)}) copy-start(f32[16,256]{1,0:T(8,128)S(1)} %log_add_fusion) | copy-start | bytes 49156
  361.3 139.0 %all-to-all-start.4 = ((bf16[4,160,1024]{2,1,0:T(8,128)(2,1)}), bf16[4,160,1024]{2,1,0:T(8,128)(2,1)S(1)}, u32[]{:S(2)}, u32[]{:S(2)}) async-start(bf16[4,160,1024]{2,1,0:T(8,128)(2,1)} %bitcast.286), calls=%async_computation.4 | async-start | bytes 2621440 | tf_op jit(solution)/shard_map/all_to_all | solution.py:173
  500.2 18.8 %copy-start.41 = (bf16[4,160,1024]{2,1,0:T(8,128)(2,1)}, bf16[4,160,1024]{2,1,0:T(8,128)(2,1)S(1)}, u32[]{:S(2)}) copy-start(bf16[4,160,1024]{2,1,0:T(8,128)(2,1)S(1)} %all-to-all-done.4) | copy-start | bytes 3932164
  534.5 20.8 %all-to-all-start.5 = ((bf16[4,160,1024]{2,1,0:T(8,128)(2,1)}), bf16[4,160,1024]{2,1,0:T(8,128)(2,1)S(1)}, u32[]{:S(2)}, u32[]{:S(2)}) async-start(bf16[4,160,1024]{2,1,0:T(8,128)(2,1)} %bitcast.289), calls=%async_computation.5 | async-start | bytes 2621440 | tf_op jit(solution)/shard_map/all_to_all | solution.py:187
  555.3 21.8 %all-to-all-start.1 = ((bf16[4,160,1024]{2,1,0:T(8,128)(2,1)}), bf16[4,160,1024]{2,1,0:T(8,128)(2,1)}, u32[]{:S(2)}, u32[]{:S(2)}) async-start(bf16[4,160,1024]{2,1,0:T(8,128)(2,1)} %bitcast.285), calls=%async_computation.1 | async-start | bytes 2621440 | tf_op jit(solution)/shard_map/all_to_all | solution.py:154
  559.8 11.1 copy-start.25
  559.8 11.1 copy-start.37
  580.9 27.7 %copy-start.55 = (f32[256,4]{0,1:T(4,128)}, f32[256,4]{0,1:T(4,128)S(1)}, u32[]{:S(2)}) copy-start(f32[256,4]{0,1:T(4,128)S(1)} %select_reduce_fusion.1) | copy-start | bytes 12292
  581.0 11.8 copy-start.69
  587.1 21.6 %all-to-all-start.2 = ((bf16[4,160,1024]{2,1,0:T(8,128)(2,1)}), bf16[4,160,1024]{2,1,0:T(8,128)(2,1)}, u32[]{:S(2)}, u32[]{:S(2)}) async-start(bf16[4,160,1024]{2,1,0:T(8,128)(2,1)} %bitcast.267), calls=%async_computation.2 | async-start | bytes 2621440 | tf_op jit(solution)/shard_map/all_to_all | solution.py:147
  592.8 117.7 %copy-start.63 = (f32[256]{0:T(256)}, f32[256]{0:T(256)S(1)}, u32[]{:S(2)}) copy-start(f32[256]{0:T(256)S(1)} %fusion.149) | copy-start | bytes 3076
  608.7 22.0 %all-to-all-start.6 = ((bf16[4,160,1024]{2,1,0:T(8,128)(2,1)}), bf16[4,160,1024]{2,1,0:T(8,128)(2,1)}, u32[]{:S(2)}, u32[]{:S(2)}) async-start(bf16[4,160,1024]{2,1,0:T(8,128)(2,1)} %bitcast.287), calls=%async_computation.8 | async-start | bytes 2621440 | tf_op jit(solution)/shard_map/all_to_all | solution.py:173
  664.0 21.8 %all-to-all-start.7 = ((bf16[4,160,1024]{2,1,0:T(8,128)(2,1)}), bf16[4,160,1024]{2,1,0:T(8,128)(2,1)}, u32[]{:S(2)}, u32[]{:S(2)}) async-start(bf16[4,160,1024]{2,1,0:T(8,128)(2,1)} %bitcast.288), calls=%async_computation.9 | async-start | bytes 2621440 | tf_op jit(solution)/shard_map/all_to_all | solution.py:187
  668.5 21.6 %copy-start.74 = (f32[256]{0:T(256)S(1)}, f32[256]{0:T(256)}, u32[]{:S(2)}) copy-start(f32[256]{0:T(256)} %copy-done.73) | copy-start | bytes 3076
  668.5 21.7 %copy-start.35 = (bf16[256,640]{0,1:T(8,128)(2,1)S(1)}, bf16[256,640]{0,1:T(8,128)(2,1)}, u32[]{:S(2)}) copy-start(bf16[256,640]{0,1:T(8,128)(2,1)} %fusion.121) | copy-start | bytes 983044
  685.8 21.6 %all-to-all-start.3 = ((bf16[4,160,1024]{2,1,0:T(8,128)(2,1)}), bf16[4,160,1024]{2,1,0:T(8,128)(2,1)}, u32[]{:S(2)}, u32[]{:S(2)}) async-start(bf16[4,160,1024]{2,1,0:T(8,128)(2,1)} %bitcast.284), calls=%async_computation.3 | async-start | bytes 2621440 | tf_op jit(solution)/shard_map/all_to_all | solution.py:154
  690.1 120.7 %reduce-scatter.21.cloned.1.call-start = ((), (), s32[]{:S(2)}) async-start(), calls=%async_computation.29 | async-start | bytes 2621440 | tf_op jit(solution)/shard_map/reduce_scatter | solution.py:248
  726.0 84.9 %reduce-scatter.19.cloned.1.call-start = ((), (), s32[]{:S(2)}) async-start(), calls=%async_computation.28 | async-start | bytes 2621440 | tf_op jit(solution)/shard_map/reduce_scatter | solution.py:242
  748.6 73.9 %reduce-scatter.17.cloned.1.call-start = ((), (), s32[]{:S(2)}) async-start(), calls=%async_computation.27 | async-start | bytes 2621440 | tf_op jit(solution)/shard_map/reduce_scatter | solution.py:248
  761.0 95.6 %reduce-scatter.15.cloned.1.call-start = ((), (), s32[]{:S(2)}) async-start(), calls=%async_computation.26 | async-start | bytes 2621440 | tf_op jit(solution)/shard_map/reduce_scatter | solution.py:242
  783.8 10.2 copy-start.54
  783.8 10.4 copy-start.64
  783.8 10.4 copy-start.72
  783.8 230.7 %reduce-scatter.33.cloned.1.call-start = ((), (), s32[]{:S(2)}) async-start(), calls=%async_computation.35 | async-start | bytes 540672
  810.7 45.9 %copy-start.8 = (bf16[2,256,1024]{2,1,0:T(8,128)(2,1)S(1)}, bf16[2,256,1024]{2,1,0:T(8,128)(2,1)}, u32[]{:S(2)}) copy-start(bf16[2,256,1024]{2,1,0:T(8,128)(2,1)} %param.11) | copy-start | bytes 3145732
  810.7 45.9 %copy-start.40 = (bf16[16,64,256]{2,1,0:T(8,128)(2,1)S(1)}, bf16[16,64,256]{2,1,0:T(8,128)(2,1)}, u32[]{:S(2)}) copy-start(bf16[16,64,256]{2,1,0:T(8,128)(2,1)} %fusion.82) | copy-start | bytes 1572868
  810.7 45.9 %copy-start.46 = (f32[1024,1]{0,1:T(1,128)S(1)}, f32[1024,1]{0,1:T(1,128)}, u32[]{:S(2)}) copy-start(f32[1024,1]{0,1:T(1,128)} %copy-done.45) | copy-start | bytes 12292
  810.7 45.9 %copy-start.60 = (f32[256]{0:T(256)S(1)}, f32[256]{0:T(256)}, u32[]{:S(2)}) copy-start(f32[256]{0:T(256)} %copy-done.59) | copy-start | bytes 3076
  810.7 45.9 %copy-start.66 = (f32[256]{0:T(256)S(1)}, f32[256]{0:T(256)}, u32[]{:S(2)}) copy-start(f32[256]{0:T(256)} %copy-done.65) | copy-start | bytes 3076
  810.8 318.4 %reduce-scatter.31.cloned.1.call-start = ((), (), s32[]{:S(2)}) async-start(), calls=%async_computation.34 | async-start | bytes 540672
  864.0 375.2 %reduce-scatter.29.cloned.1.call-start = ((), (), s32[]{:S(2)}) async-start(), calls=%async_computation.33 | async-start | bytes 6488064 | tf_op jit(solution)/shard_map/reduce_scatter | solution.py:282
  877.3 557.6 %reduce-scatter.27.cloned.1.call-start = ((), (), s32[]{:S(2)}) async-start(), calls=%async_computation.32 | async-start | bytes 12976128 | tf_op jit(solution)/shard_map/reduce_scatter | solution.py:279
  917.7 661.2 %reduce-scatter.25.cloned.1.call-start = ((), (), s32[]{:S(2)}) async-start(), calls=%async_computation.31 | async-start | bytes 4325376 | tf_op jit(solution)/shard_map/reduce_scatter | solution.py:271
  923.5 812.6 %reduce-scatter.23.cloned.1.call-start = ((), (), s32[]{:S(2)}) async-start(), calls=%async_computation.30 | async-start | bytes 12976128 | tf_op jit(solution)/shard_map/reduce_scatter | solution.py:270
  966.9 49.1 %copy-start.76 = (f32[256]{0:T(256)S(1)}, f32[256]{0:T(256)}, u32[]{:S(2)}) copy-start(f32[256]{0:T(256)} %copy-done.75) | copy-start | bytes 3076
  966.9 49.1 %copy-start.78 = (f32[256]{0:T(256)S(1)}, f32[256]{0:T(256)}, u32[]{:S(2)}) copy-start(f32[256]{0:T(256)} %copy-done.77) | copy-start | bytes 3076
  (45 other events, 284.0 us)
Sparse Core Ops, SparseCore 0:
  10.9 72.0 all-gather.10
  89.1 21.0 all-gather.12
  112.4 22.5 all-gather.14
  137.7 56.5 all-gather.16
  196.3 21.4 all-gather.24
  219.2 22.6 all-gather.22
  244.2 163.3 all-gather.18
  409.7 90.4 all-gather.20
  726.1 28.4 reduce-scatter.20
  757.5 31.1 reduce-scatter.18
  791.3 31.1 reduce-scatter.16
  825.4 31.1 reduce-scatter.14
  858.9 135.8 reduce-scatter.32
  997.4 131.6 reduce-scatter.30
  1132.7 106.4 reduce-scatter.28
  1242.7 192.1 reduce-scatter.26
  1437.6 141.2 reduce-scatter.24
  1585.3 150.7 reduce-scatter.22
where the time goes:
time: 1750 us; the launch traced here: 1740 us
  waiting for transfers between devices  955 us (55%)
  matrix products  398 us (23%)
  blocking collectives  163 us (9%)
  local copies, waits for them, and re-layouts  107 us (6%)
  other arithmetic  68.2 us (4%)
  starting transfers between devices  36 us (2%)
    reduce_scatter x1, waiting for transfers between devices, local(): lax.psum_scatter(acc_in[None].astype(jnp.bfloat16), 'dp', scatter_dimensi...  193 us
    reduce_scatter x1, waiting for transfers between devices, local(): lax.psum_scatter(acc_qkv, ('dp', 'expert'), scatter_dimension=0, tiled=True)  157 us
    reduce_scatter x1, waiting for transfers between devices, local(): lax.psum_scatter(acc_out, ('dp', 'expert'), scatter_dimension=0, tiled=True)  141 us
    unnamed x20, waiting for transfers between devices  114 us
    reduce_scatter x1, waiting for transfers between devices, local(): lax.psum_scatter(acc_down[None].astype(jnp.bfloat16), 'dp', scatter_dimen...  109 us
    dot_general x10, matrix products, times_trans(): jnp.einsum('ti,ji->tj', left, right, preferred_element_type=jnp.float32)  88.5 us
    dot_general x10, matrix products, inner_rows(): jnp.einsum('ti,tj->ij', left, right, preferred_element_type=jnp.float32)  79.1 us
    unnamed x2, blocking collectives  79.1 us
  transfers between devices with their start and end apart: 26, of which 16 were waited for; matrix products, arithmetic and copies ran while one was open for 27% of the time, Pallas kernels for 0%

commit v1 on v0

--- a/solution.py
+++ b/solution.py
@@ -12,6 +12,24 @@
 bucket_edges = (12, 16, 23, 32, 46, 64, 91)
 norm_eps = 1e-06
 highest = lax.Precision.HIGHEST
+
+
+def gather_around(shard, axis, dim):
+    ways, here, hop = (lax.axis_size(axis), lax.axis_index(axis), shard.shape[dim])
+    dims = [n * ways if d == dim else n for d, n in enumerate(shard.shape)]
+    full = lax.dynamic_update_slice_in_dim(
+        jnp.zeros(dims, shard.dtype), shard, here * hop, axis=dim
+    )
+    going_up = going_down = shard
+    for far in range(1, ways // 2 + 1):
+        going_up = lax.ppermute(going_up, axis, [(d, (d + 1) % ways) for d in range(ways)])
+        full = lax.dynamic_update_slice_in_dim(full, going_up, (here - far) % ways * hop, axis=dim)
+        if 2 * far < ways:
+            going_down = lax.ppermute(going_down, axis, [(d, (d - 1) % ways) for d in range(ways)])
+            full = lax.dynamic_update_slice_in_dim(
+                full, going_down, (here + far) % ways * hop, axis=dim
+            )
+    return full
 
 
 def bucket_ids(query_pos, key_pos):
@@ -92,10 +110,7 @@
                 lax.all_gather(bias_table, ("dp", "expert"), axis=0, tiled=True),
                 lax.all_gather(router, ("dp", "expert"), axis=0, tiled=True),
             ),
-            (
-                lax.all_gather(w_in, "dp", axis=1, tiled=True),
-                lax.all_gather(w_down, "dp", axis=1, tiled=True),
-            ),
+            (lax.all_gather(w_in, "dp", axis=1, tiled=True), gather_around(w_down, "dp", 1)),
         )
         gains_f = gains.astype(jnp.float32)
         table = table_flat.astype(jnp.float32).reshape(BUCKETS, H)

time: 1750 us -> 1740 us (level)
  waiting for transfers between devices: 955 us -> 902 us
  starting transfers between devices: 36 us -> 58.6 us
    all_gather x1 -> x0, waiting for transfers between devices: 79 us -> none  [local(): lax.all_gather(w_down, 'dp', axis=1, tiled=True)]
    ppermute x0 -> x7, waiting for transfers between devices: none -> 64.5 us  [the longest x3 58 us: gather_around(): lax.ppermute(going_down, axis, [(d, (d - 1) % ways) for d in range(ways)])]
    all_gather x1, waiting for transfers between devices: 42.5 us -> 0.02 us  [local(): lax.all_gather(w_in, 'dp', axis=1, tiled=True)]
    ppermute x0 -> x7, starting transfers between devices: none -> 22.7 us  [the longest x4 13.8 us: gather_around(): lax.ppermute(going_up, axis, [(d, (d + 1) % ways) for d in range(ways)])]
    unnamed x20 -> x19, waiting for transfers between devices: 114 us -> 113 us
  transfers between devices with their start and end apart: 26 -> 32, of which waited for: 16 -> 19; matrix products, arithmetic and copies ran while one was open for 27% -> 28% of each run, Pallas kernels for 0% -> 0%
where the time goes in v1:
time: 1740 us; the launch traced here: 1730 us
  waiting for transfers between devices  902 us (52%)
  matrix products  398 us (23%)
  blocking collectives  168 us (10%)
  local copies, waits for them, and re-layouts  122 us (7%)
  other arithmetic  67.2 us (4%)
  starting transfers between devices  58.6 us (3%)
    reduce_scatter x1, waiting for transfers between devices, local(): lax.psum_scatter(acc_in[None].astype(jnp.bfloat16), 'dp', scatter_dimensi...  193 us
    reduce_scatter x1, waiting for transfers between devices, local(): lax.psum_scatter(acc_qkv, ('dp', 'expert'), scatter_dimension=0, tiled=True)  157 us
    reduce_scatter x1, waiting for transfers between devices, local(): lax.psum_scatter(acc_out, ('dp', 'expert'), scatter_dimension=0, tiled=True)  141 us
    unnamed x19, waiting for transfers between devices  113 us
    reduce_scatter x1, waiting for transfers between devices, local(): lax.psum_scatter(acc_down[None].astype(jnp.bfloat16), 'dp', scatter_dimen...  109 us
    dot_general x10, matrix products, times_trans(): jnp.einsum('ti,ji->tj', left, right, preferred_element_type=jnp.float32)  88.4 us
    dot_general x10, matrix products, inner_rows(): jnp.einsum('ti,tj->ij', left, right, preferred_element_type=jnp.float32)  79 us
    unnamed x2, blocking collectives  77.6 us
  transfers between devices with their start and end apart: 32, of which 19 were waited for; matrix products, arithmetic and copies ran while one was open for 28% of the time, Pallas kernels for 0%

profile of v1, /device:TPU:0, one launch (start us, length us, event | category | flops | bytes accessed | tf_op | source)
XLA Modules:
  0.0 1730.7 jit_solution(17359545642670387388)
XLA Ops:
  8.0 43.5 %all-gather = bf16[32,32,2]{1,2,0:T(2,128)(2,1)S(1)} all-gather(bf16[1,32,2]{1,2,0:T(2,128)(2,1)} %bitcast.312), channel_id=1, replica_groups=mesh['dp'=8,'expert'=4] {'dp','expert'}, dimensions={0}, use_global_device_ids=true | all-gather | bytes 4224 | tf_op jit(solution)/shard_map/all_gather | solution.py:109
  53.6 29.3 %all-gather.10.cloned.1.call-done = bf16[1024,3072]{1,0:T(8,128)(2,1)} async-done(((bf16[32,3072]{1,0:T(8,128)(2,1)}), bf16[1024,3072]{1,0:T(8,128)(2,1)}) %all-gather.10.cloned.1.call-update) | async-done | bytes 6291472 | tf_op jit(solution)/shard_map/all_gather | solution.py:107
  82.9 4.9 convolution_convert_fusion.1
  90.4 4.7 convolution_convert_fusion
  104.5 7.9 iota_compare_fusion
  112.4 46.0 %copy.135 = pred[256,1024,32]{1,2,0:T(32,128)(4,1)} copy(pred[256,1024,32]{0,2,1:T(32,128)(4,1)} %iota_compare_fusion) | data formatting | bytes 16777216 | tf_op jit(solution)/shard_map/eq | solution.py:91
  158.7 38.2 %all-reduce.4 = bf16[512]{0:T(512)(128)(2,1)S(1)} all-reduce(bf16[512]{0:T(512)(128)(2,1)S(1)} %dynamic-update-slice), channel_id=1, replica_groups=mesh['dp'=8,'expert'=4] {'dp','expert'}, use_global_device_ids=true, to_apply=%add.4 | all-reduce | flops 512 | bytes 2048
  206.4 10.2 fusion.128
  220.8 46.8 %all-gather.1 = bf16[32,32,4]{1,2,0:T(4,128)(2,1)S(1)} all-gather(bf16[1,32,4]{1,2,0:T(4,128)(2,1)S(1)} %bitcast.311), channel_id=1, replica_groups=mesh['dp'=8,'expert'=4] {'dp','expert'}, dimensions={0}, use_global_device_ids=true | all-gather | bytes 8448 | tf_op jit(solution)/shard_map/all_gather | solution.py:111
  281.9 21.0 %collective-permute-done.3 = bf16[1,352,1024]{2,1,0:T(8,128)(2,1)S(1)} collective-permute-done((bf16[1,352,1024]{2,1,0:T(8,128)(2,1)}, bf16[1,352,1024]{2,1,0:T(8,128)(2,1)S(1)}, u32[]{:S(2)}, u32[]{:S(2)}) %collective-permute-start.3) | collective-permute-done | bytes 720928 | tf_op jit(solution)/shard_map/ppermute | solution.py:28
  302.9 5.1 collective-permute-start.5
  313.1 8.3 collective-permute-start.6
  323.2 37.0 %collective-permute-done.5 = bf16[1,352,1024]{2,1,0:T(8,128)(2,1)S(1)} collective-permute-done((bf16[1,352,1024]{2,1,0:T(8,128)(2,1)S(1)}, bf16[1,352,1024]{2,1,0:T(8,128)(2,1)S(1)}, u32[]{:S(2)}, u32[]{:S(2)}) %collective-permute-start.5) | collective-permute-done | bytes 720928 | tf_op jit(solution)/shard_map/ppermute | solution.py:28
  374.3 22.4 %fusion.157 = (f32[16,256]{1,0:T(8,128)S(1)}, f32[16,256,1024]{2,1,0:T(8,128)}) fusion(f32[16,256,1024]{2,0,1:T(8,128)} %fusion.128, bf16[256,16,64]{0,2,1:T(8,128)(2,1)} %bitcast.263, bf16[1024,16,64]{0,2,1:T(8,128)(2,1)S(1)} %bitcast.253, pred[1024]{0:T(1024)(128)(4,1)S(1)} %iota_compare_fusion.22), kind=kOutput, calls=%fused_computation.267 | convolution fusion | flops 553644032 | bytes 36193280 | tf_op jit(solution)/shard_map/qhd,khd->hqk/dot_general | solution.py:135
  396.7 7.9 exponential_reduce_fusion.1
  404.7 8.5 fusion.62
  419.6 4.5 all-to-all-start
  427.0 22.4 %fusion.159 = (f32[16,256]{1,0:T(8,128)S(1)}, f32[16,256,1024]{2,1,0:T(8,128)}) fusion(f32[16,256,1024]{2,0,1:T(8,128)} %fusion.128, bf16[256,16,64]{0,2,1:T(8,128)(2,1)} %bitcast.265, bf16[1024,16,64]{0,2,1:T(8,128)(2,1)S(1)} %bitcast.255, pred[1024]{0:T(1024)(128)(4,1)S(1)} %iota_compare_fusion.21), kind=kOutput, calls=%fused_computation.269 | convolution fusion | flops 553644032 | bytes 36193280 | tf_op jit(solution)/shard_map/qhd,khd->hqk/dot_general | solution.py:135
  449.4 7.8 exponential_reduce_fusion
  469.2 13.7 fusion.12
  486.3 18.8 %fusion.28 = (f32[640,2816]{1,0:T(8,128)}, f32[640,2816]{1,0:T(8,128)}, bf16[640,2816]{1,0:T(8,128)(2,1)}) fusion(f32[640,5632]{1,0:T(8,128)} %fusion.12, bf16[640,1024]{1,0:T(8,128)(2,1)S(1)} %bitcast.285, bf16[2816,1024]{1,0:T(8,128)(2,1)} %bitcast_dynamic-update-slice_fusion), kind=kOutput, calls=%fused_computation.59 | convolution fusion | flops 3734241280 | bytes 39518208 | tf_op jit(solution)/shard_map/ti,ji->tj/dot_general | solution.py:77
  505.1 15.5 fusion.52
  524.2 8.7 convolution_convert_fusion.5
  532.9 8.5 all-to-all-done.5
  541.4 4.7 all-to-all-start.1
  546.1 9.3 fusion.65
  558.8 4.6 all-to-all-done.1
  580.0 4.9 bitcast_convert_fusion
  585.0 10.9 all-to-all-done.2
  595.8 4.5 all-to-all-start.6
  600.3 13.8 fusion.10
  617.6 17.9 %fusion.29 = (f32[640,2816]{1,0:T(8,128)}, f32[640,2816]{1,0:T(8,128)}, bf16[640,2816]{1,0:T(8,128)(2,1)}) fusion(f32[640,5632]{1,0:T(8,128)} %fusion.10, bf16[640,1024]{1,0:T(8,128)(2,1)} %bitcast.65, bf16[2816,1024]{1,0:T(8,128)(2,1)} %bitcast_dynamic-update-slice_fusion), kind=kOutput, calls=%fused_computation.60 | convolution fusion | flops 3734241280 | bytes 39518208 | tf_op jit(solution)/shard_map/ti,ji->tj/dot_general | solution.py:77
  635.5 15.5 fusion.55
  651.0 4.5 all-to-all-start.7
  655.5 8.7 convolution_convert_fusion.4
  664.2 8.6 all-to-all-done.7
  680.1 14.3 all-to-all-done.3
  703.8 9.0 fusion.45
  712.9 9.8 multiply_reduce_fusion
  722.7 8.0 multiply_convert_fusion
  738.7 9.4 fusion.42
  748.1 10.7 multiply_reduce_fusion.1
  758.8 7.8 multiply_convert_fusion.1
  770.9 9.6 fusion.164
  782.0 7.9 fusion.69
  789.9 6.9 fusion.68
  797.0 6.2 fusion.112
  803.2 7.0 reduce-scatter.17.cloned.1.call-done
  810.2 34.3 %reduce-scatter.15.cloned.1.call-done = bf16[256,1024]{0,1:T(8,128)(2,1)} async-done(((bf16[1024,1024]{0,1:T(8,128)(2,1)}), bf16[256,1024]{0,1:T(8,128)(2,1)}) %reduce-scatter.15.cloned.1.call-update) | async-done | bytes 524304 | tf_op jit(solution)/shard_map/reduce_scatter | solution.py:257
  844.5 6.3 fusion.80
  852.3 13.0 fusion.27
  865.3 19.0 %fusion.105 = f32[1024,5632]{1,0:T(8,128)} fusion(bf16[640,1024]{1,0:T(8,128)(2,1)} %bitcast.17, f32[640,2816]{1,0:T(8,128)} %get-tuple-element.26, f32[640,2816]{1,0:T(8,128)} %get-tuple-element.25), kind=kOutput, calls=%fused_computation.163 | convolution fusion | flops 7389184000 | bytes 38797312 | tf_op jit(solution)/shard_map/ti,tj->ij/dot_general | solution.py:73
  884.3 21.2 %fusion.14 = bf16[1,1024,5632]{2,1,0:T(8,128)(2,1)} fusion(f32[1024,5632]{1,0:T(8,128)} %fusion.105, bf16[640,1024]{1,0:T(8,128)(2,1)} %bitcast.43, f32[640,2816]{1,0:T(8,128)} %get-tuple-element.28, f32[640,2816]{1,0:T(8,128)} %get-tuple-element.27), kind=kOutput, calls=%fused_computation.33 | convolution fusion | flops 7400718336 | bytes 50331648 | tf_op jit(solution)/shard_map/ti,tj->ij/dot_general | solution.py:73
  915.1 6.7 convolution_add_fusion
  921.9 12.7 copy.156
  934.5 12.5 copy.157
  947.1 7.6 fusion.74
  954.7 5.3 fusion.76
  960.2 39.4 %all-reduce.5 = f32[512]{0:T(512)S(1)} all-reduce(f32[512]{0:T(512)S(1)} %reshape.503), channel_id=9, replica_groups=mesh['dp'=8,'expert'=4] {'dp','expert'}, use_global_device_ids=true, to_apply=%region_47.48.clone | all-reduce | flops 512 | bytes 4096
  1007.5 109.5 %reduce-scatter.31.cloned.1.call-done = f32[32,2]{1,0:T(8,128)} async-done(((f32[1024,2]{1,0:T(8,128)}), f32[32,2]{1,0:T(8,128)}) %reduce-scatter.31.cloned.1.call-update) | async-done | bytes 272
  1118.4 108.7 %reduce-scatter.29.cloned.1.call-done = bf16[1,352,1024]{2,1,0:T(8,128)(2,1)} async-done(((bf16[1,2816,1024]{2,1,0:T(8,128)(2,1)}), bf16[1,352,1024]{2,1,0:T(8,128)(2,1)}) %reduce-scatter.29.cloned.1.call-update) | async-done | bytes 720912 | tf_op jit(solution)/shard_map/reduce_scatter | solution.py:297
  1229.5 193.3 %reduce-scatter.27.cloned.1.call-done = bf16[1,128,5632]{2,1,0:T(8,128)(2,1)} async-done(((bf16[1,1024,5632]{2,1,0:T(8,128)(2,1)}), bf16[1,128,5632]{2,1,0:T(8,128)(2,1)}) %reduce-scatter.27.cloned.1.call-update) | async-done | bytes 1441808 | tf_op jit(solution)/shard_map/reduce_scatter | solution.py:294
  1426.0 140.8 %reduce-scatter.25.cloned.1.call-done = f32[32,1024]{1,0:T(8,128)} async-done(((f32[1024,1024]{1,0:T(8,128)}), f32[32,1024]{1,0:T(8,128)}) %reduce-scatter.25.cloned.1.call-update) | async-done | bytes 131088 | tf_op jit(solution)/shard_map/reduce_scatter | solution.py:286
  1566.8 157.2 %reduce-scatter.23.cloned.1.call-done = f32[32,3072]{1,0:T(8,128)} async-done(((f32[1024,3072]{1,0:T(8,128)}), f32[32,3072]{1,0:T(8,128)}) %reduce-scatter.23.cloned.1.call-update) | async-done | bytes 393232 | tf_op jit(solution)/shard_map/reduce_scatter | solution.py:285
  (359 shorter events, 171.4 us)
Async XLA Ops:
  7.2 75.8 %all-gather.10.cloned.1.call-start = ((), (), s32[]{:S(2)}) async-start(), calls=%async_computation.18 | async-start | bytes 6488064 | tf_op jit(solution)/shard_map/all_gather | solution.py:107
  7.9 359.6 %all-gather.12.cloned.1.call-start = ((), (), s32[]{:S(2)}) async-start(), calls=%async_computation.19 | async-start | bytes 2621440 | tf_op jit(solution)/shard_map/all_gather | solution.py:127
  53.0 37.4 %copy-start.76 = (f32[256]{0:T(256)}, f32[256]{0:T(256)S(1)}, u32[]{:S(2)}) copy-start(f32[256]{0:T(256)S(1)} %get-tuple-element.24) | copy-start | bytes 3076
  53.6 34.3 %copy-start.58 = (f32[256]{0:T(256)}, f32[256]{0:T(256)S(1)}, u32[]{:S(2)}) copy-start(f32[256]{0:T(256)S(1)} %fusion.140) | copy-start | bytes 3076
  53.6 36.8 %copy-start.44 = (f32[1024,1]{0,1:T(1,128)}, f32[1024,1]{0,1:T(1,128)S(1)}, u32[]{:S(2)}) copy-start(f32[1024,1]{0,1:T(1,128)S(1)} %get-tuple-element.46) | copy-start | bytes 12292
  89.0 282.4 %all-gather.14.cloned.1.call-start = ((), (), s32[]{:S(2)}) async-start(), calls=%async_computation.20 | async-start | bytes 2621440 | tf_op jit(solution)/shard_map/all_gather | solution.py:126
  89.7 323.5 %all-gather.16.cloned.1.call-start = ((), (), s32[]{:S(2)}) async-start(), calls=%async_computation.21 | async-start | bytes 2162688 | tf_op jit(solution)/shard_map/all_gather | solution.py:108
  90.3 333.8 %all-gather.22.cloned.1.call-start = ((), (), s32[]{:S(2)}) async-start(), calls=%async_computation.24 | async-start | bytes 2621440 | tf_op jit(solution)/shard_map/all_gather | solution.py:126
  90.4 12.1 copy-start.78
  96.3 361.3 %all-gather.20.cloned.1.call-start = ((), (), s32[]{:S(2)}) async-start(), calls=%async_computation.23 | async-start | bytes 2621440 | tf_op jit(solution)/shard_map/all_gather | solution.py:127
  96.9 372.3 %all-gather.18.cloned.1.call-start = ((), (), s32[]{:S(2)}) async-start(), calls=%async_computation.22 | async-start | bytes 12976128 | tf_op jit(solution)/shard_map/all_gather | solution.py:113
  97.6 120.1 %collective-permute-start = (bf16[1,352,1024]{2,1,0:T(8,128)(2,1)}, bf16[1,352,1024]{2,1,0:T(8,128)(2,1)}, u32[]{:S(2)}, u32[]{:S(2)}) collective-permute-start(bf16[1,352,1024]{2,1,0:T(8,128)(2,1)} %param.20), channel_id=1, source_target_pairs={{0,4},{4,8},{8,12},{12,16},{16,20},{20,24},{24,28},{28,0},{1,5},{5... | collective-permute-start | bytes 2162696 | tf_op jit(solution)/shard_map/ppermute | solution.py:25
  99.1 171.4 %collective-permute-start.1 = (bf16[1,352,1024]{2,1,0:T(8,128)(2,1)}, bf16[1,352,1024]{2,1,0:T(8,128)(2,1)}, u32[]{:S(2)}, u32[]{:S(2)}) collective-permute-start(bf16[1,352,1024]{2,1,0:T(8,128)(2,1)} %param.20), channel_id=1, source_target_pairs={{0,28},{4,0},{8,4},{12,8},{16,12},{20,16},{24,20},{28,24},{1,29},{... | collective-permute-start | bytes 2162696 | tf_op jit(solution)/shard_map/ppermute | solution.py:28
  103.1 103.2 %copy-start.34 = (s32[1,256,2]{2,1,0:T(8,128)}, s32[1,256,2]{2,1,0:T(8,128)S(1)}, u32[]{:S(2)}) copy-start(s32[1,256,2]{2,1,0:T(8,128)S(1)} %copy.168) | copy-start | bytes 6148
  104.5 53.9 %copy-start.32 = (s32[256,1024]{0,1:T(8,128)}, s32[256,1024]{0,1:T(8,128)S(1)}, u32[]{:S(2)}) copy-start(s32[256,1024]{0,1:T(8,128)S(1)} %fusion.91) | copy-start | bytes 3145732
  112.4 46.0 %copy-start.81 = (bf16[16]{0:T(256)(128)(2,1)S(1)}, bf16[16]{0:T(256)(128)(2,1)}, u32[]{:S(2)}) copy-start(bf16[16]{0:T(256)(128)(2,1)} %param.17) | copy-start | bytes 100
  112.4 84.6 %copy-start.79 = (s32[2,1]{0,1:T(1,128)S(1)}, s32[2,1]{0,1:T(1,128)}, u32[]{:S(2)}) copy-start(s32[2,1]{0,1:T(1,128)} %param.12) | copy-start | bytes 28
  206.4 14.4 copy-start.80
  206.4 62.5 %copy-start.29 = (bf16[2,256,1024]{2,1,0:T(8,128)(2,1)S(1)}, bf16[2,256,1024]{2,1,0:T(8,128)(2,1)}, u32[]{:S(2)}) copy-start(bf16[2,256,1024]{2,1,0:T(8,128)(2,1)} %param.21) | copy-start | bytes 3145732
  217.7 58.4 %collective-permute-start.2 = (bf16[1,352,1024]{2,1,0:T(8,128)(2,1)}, bf16[1,352,1024]{2,1,0:T(8,128)(2,1)}, u32[]{:S(2)}, u32[]{:S(2)}) collective-permute-start(bf16[1,352,1024]{2,1,0:T(8,128)(2,1)} %collective-permute-done), channel_id=1, source_target_pairs={{0,4},{4,8},{8,12},{12,16},{16,20},{20,24},{24,28},{28,0},{1,5},{5... | collective-permute-start | bytes 2162696 | tf_op jit(solution)/shard_map/ppermute | solution.py:25
  270.5 32.4 %collective-permute-start.3 = (bf16[1,352,1024]{2,1,0:T(8,128)(2,1)}, bf16[1,352,1024]{2,1,0:T(8,128)(2,1)S(1)}, u32[]{:S(2)}, u32[]{:S(2)}) collective-permute-start(bf16[1,352,1024]{2,1,0:T(8,128)(2,1)} %collective-permute-done.1), channel_id=1, source_target_pairs={{0,28},{4,0},{8,4},{12,8},{16,12},{20,16},{24,20},{28,24},{1,29},{... | collective-permute-start | bytes 2162696 | tf_op jit(solution)/shard_map/ppermute | solution.py:28
  274.0 92.5 %copy-start.38 = (bf16[256,1024]{1,0:T(8,128)(2,1)S(1)}, bf16[256,1024]{1,0:T(8,128)(2,1)}, u32[]{:S(2)}) copy-start(bf16[256,1024]{1,0:T(8,128)(2,1)} %get-tuple-element.35) | copy-start | bytes 1572868
  276.1 37.0 %collective-permute-start.4 = (bf16[1,352,1024]{2,1,0:T(8,128)(2,1)}, bf16[1,352,1024]{2,1,0:T(8,128)(2,1)S(1)}, u32[]{:S(2)}, u32[]{:S(2)}) collective-permute-start(bf16[1,352,1024]{2,1,0:T(8,128)(2,1)} %collective-permute-done.2), channel_id=1, source_target_pairs={{0,4},{4,8},{8,12},{12,16},{16,20},{20,24},{24,28},{28,0},{1,5},{5... | collective-permute-start | bytes 2162696 | tf_op jit(solution)/shard_map/ppermute | solution.py:25
  302.9 57.4 %collective-permute-start.5 = (bf16[1,352,1024]{2,1,0:T(8,128)(2,1)S(1)}, bf16[1,352,1024]{2,1,0:T(8,128)(2,1)S(1)}, u32[]{:S(2)}, u32[]{:S(2)}) collective-permute-start(bf16[1,352,1024]{2,1,0:T(8,128)(2,1)S(1)} %collective-permute-done.3), channel_id=1, source_target_pairs={{0,28},{4,0},{8,4},{12,8},{16,12},{20,16},{24,20},{28,24},{1,29},{... | collective-permute-start | bytes 2162696 | tf_op jit(solution)/shard_map/ppermute | solution.py:28
  313.1 51.4 %collective-permute-start.6 = (bf16[1,352,1024]{2,1,0:T(8,128)(2,1)S(1)}, bf16[1,352,1024]{2,1,0:T(8,128)(2,1)S(1)}, u32[]{:S(2)}, u32[]{:S(2)}) collective-permute-start(bf16[1,352,1024]{2,1,0:T(8,128)(2,1)S(1)} %collective-permute-done.4), channel_id=1, source_target_pairs={{0,4},{4,8},{8,12},{12,16},{16,20},{20,24},{24,28},{28,0},{1,5},{5... | collective-permute-start | bytes 2162696 | tf_op jit(solution)/shard_map/ppermute | solution.py:25
  374.3 22.4 %copy-start.4 = (bf16[1024,1024]{0,1:T(8,128)(2,1)}, bf16[1024,1024]{0,1:T(8,128)(2,1)S(1)}, u32[]{:S(2)}) copy-start(bf16[1024,1024]{0,1:T(8,128)(2,1)S(1)} %copy.133) | copy-start | bytes 6291460
  416.1 33.3 %copy-start.72 = (f32[256]{0:T(256)}, f32[256]{0:T(256)S(1)}, u32[]{:S(2)}) copy-start(f32[256]{0:T(256)S(1)} %get-tuple-element.54) | copy-start | bytes 3076
  419.6 45.8 %all-to-all-start = ((bf16[4,160,1024]{2,1,0:T(8,128)(2,1)}), bf16[4,160,1024]{2,1,0:T(8,128)(2,1)}, u32[]{:S(2)}, u32[]{:S(2)}) async-start(bf16[4,160,1024]{2,1,0:T(8,128)(2,1)} %bitcast.16), calls=%async_computation | async-start | bytes 2621440 | tf_op jit(solution)/shard_map/all_to_all | solution.py:162
  427.0 22.5 %copy-start.6 = (bf16[1024,1024]{0,1:T(8,128)(2,1)}, bf16[1024,1024]{0,1:T(8,128)(2,1)S(1)}, u32[]{:S(2)}) copy-start(bf16[1024,1024]{0,1:T(8,128)(2,1)S(1)} %copy.146) | copy-start | bytes 6291460
  449.4 12.2 copy-start.42
  457.5 109.7 %copy-start.52 = (f32[256,4]{0,1:T(4,128)}, f32[256,4]{0,1:T(4,128)S(1)}, u32[]{:S(2)}) copy-start(f32[256,4]{0,1:T(4,128)S(1)} %get-tuple-element.57) | copy-start | bytes 12292
  457.5 109.7 %copy-start.56 = (f32[256]{0:T(256)}, f32[256]{0:T(256)S(1)}, u32[]{:S(2)}) copy-start(f32[256]{0:T(256)S(1)} %get-tuple-element.56) | copy-start | bytes 3076
  461.5 105.7 %copy-start.60 = (f32[256]{0:T(256)}, f32[256]{0:T(256)S(1)}, u32[]{:S(2)}) copy-start(f32[256]{0:T(256)S(1)} %fusion.133) | copy-start | bytes 3076
  461.6 84.5 %copy-start.50 = (f32[16,256]{1,0:T(8,128)}, f32[16,256]{1,0:T(8,128)S(1)}, u32[]{:S(2)}) copy-start(f32[16,256]{1,0:T(8,128)S(1)} %log_add_fusion) | copy-start | bytes 49156
  465.4 20.9 %all-to-all-start.4 = ((bf16[4,160,1024]{2,1,0:T(8,128)(2,1)}), bf16[4,160,1024]{2,1,0:T(8,128)(2,1)S(1)}, u32[]{:S(2)}, u32[]{:S(2)}) async-start(bf16[4,160,1024]{2,1,0:T(8,128)(2,1)} %bitcast.289), calls=%async_computation.4 | async-start | bytes 2621440 | tf_op jit(solution)/shard_map/all_to_all | solution.py:188
  486.3 18.8 %copy-start.40 = (bf16[4,160,1024]{2,1,0:T(8,128)(2,1)}, bf16[4,160,1024]{2,1,0:T(8,128)(2,1)S(1)}, u32[]{:S(2)}) copy-start(bf16[4,160,1024]{2,1,0:T(8,128)(2,1)S(1)} %all-to-all-done.4) | copy-start | bytes 3932164
  520.6 20.8 %all-to-all-start.5 = ((bf16[4,160,1024]{2,1,0:T(8,128)(2,1)}), bf16[4,160,1024]{2,1,0:T(8,128)(2,1)S(1)}, u32[]{:S(2)}, u32[]{:S(2)}) async-start(bf16[4,160,1024]{2,1,0:T(8,128)(2,1)} %bitcast.292), calls=%async_computation.5 | async-start | bytes 2621440 | tf_op jit(solution)/shard_map/all_to_all | solution.py:202
  541.4 22.0 %all-to-all-start.1 = ((bf16[4,160,1024]{2,1,0:T(8,128)(2,1)}), bf16[4,160,1024]{2,1,0:T(8,128)(2,1)}, u32[]{:S(2)}, u32[]{:S(2)}) async-start(bf16[4,160,1024]{2,1,0:T(8,128)(2,1)} %bitcast.288), calls=%async_computation.1 | async-start | bytes 2621440 | tf_op jit(solution)/shard_map/all_to_all | solution.py:169
  563.4 15.2 copy-start.35
  567.2 17.8 %copy-start.54 = (f32[256,4]{0,1:T(4,128)}, f32[256,4]{0,1:T(4,128)S(1)}, u32[]{:S(2)}) copy-start(f32[256,4]{0,1:T(4,128)S(1)} %select_reduce_fusion.1) | copy-start | bytes 12292
  574.2 21.6 %all-to-all-start.2 = ((bf16[4,160,1024]{2,1,0:T(8,128)(2,1)}), bf16[4,160,1024]{2,1,0:T(8,128)(2,1)}, u32[]{:S(2)}, u32[]{:S(2)}) async-start(bf16[4,160,1024]{2,1,0:T(8,128)(2,1)} %bitcast.270), calls=%async_computation.2 | async-start | bytes 2621440 | tf_op jit(solution)/shard_map/all_to_all | solution.py:162
  580.0 117.5 %copy-start.62 = (f32[256]{0:T(256)}, f32[256]{0:T(256)S(1)}, u32[]{:S(2)}) copy-start(f32[256]{0:T(256)S(1)} %fusion.135) | copy-start | bytes 3076
  595.8 21.8 %all-to-all-start.6 = ((bf16[4,160,1024]{2,1,0:T(8,128)(2,1)}), bf16[4,160,1024]{2,1,0:T(8,128)(2,1)}, u32[]{:S(2)}, u32[]{:S(2)}) async-start(bf16[4,160,1024]{2,1,0:T(8,128)(2,1)} %bitcast.290), calls=%async_computation.8 | async-start | bytes 2621440 | tf_op jit(solution)/shard_map/all_to_all | solution.py:188
  651.0 21.8 %all-to-all-start.7 = ((bf16[4,160,1024]{2,1,0:T(8,128)(2,1)}), bf16[4,160,1024]{2,1,0:T(8,128)(2,1)}, u32[]{:S(2)}, u32[]{:S(2)}) async-start(bf16[4,160,1024]{2,1,0:T(8,128)(2,1)} %bitcast.291), calls=%async_computation.9 | async-start | bytes 2621440 | tf_op jit(solution)/shard_map/all_to_all | solution.py:202
  655.5 21.6 %copy-start.73 = (f32[256]{0:T(256)S(1)}, f32[256]{0:T(256)}, u32[]{:S(2)}) copy-start(f32[256]{0:T(256)} %copy-done.72) | copy-start | bytes 3076
  655.5 21.7 %copy-start.36 = (bf16[256,640]{0,1:T(8,128)(2,1)S(1)}, bf16[256,640]{0,1:T(8,128)(2,1)}, u32[]{:S(2)}) copy-start(bf16[256,640]{0,1:T(8,128)(2,1)} %fusion.107) | copy-start | bytes 983044
  672.8 21.6 %all-to-all-start.3 = ((bf16[4,160,1024]{2,1,0:T(8,128)(2,1)}), bf16[4,160,1024]{2,1,0:T(8,128)(2,1)}, u32[]{:S(2)}, u32[]{:S(2)}) async-start(bf16[4,160,1024]{2,1,0:T(8,128)(2,1)} %bitcast.287), calls=%async_computation.3 | async-start | bytes 2621440 | tf_op jit(solution)/shard_map/all_to_all | solution.py:169
  677.1 119.8 %reduce-scatter.21.cloned.1.call-start = ((), (), s32[]{:S(2)}) async-start(), calls=%async_computation.28 | async-start | bytes 2621440 | tf_op jit(solution)/shard_map/reduce_scatter | solution.py:263
  712.9 84.1 %reduce-scatter.19.cloned.1.call-start = ((), (), s32[]{:S(2)}) async-start(), calls=%async_computation.27 | async-start | bytes 2621440 | tf_op jit(solution)/shard_map/reduce_scatter | solution.py:257
  735.4 74.8 %reduce-scatter.17.cloned.1.call-start = ((), (), s32[]{:S(2)}) async-start(), calls=%async_computation.26 | async-start | bytes 2621440 | tf_op jit(solution)/shard_map/reduce_scatter | solution.py:263
  748.1 96.4 %reduce-scatter.15.cloned.1.call-start = ((), (), s32[]{:S(2)}) async-start(), calls=%async_computation.25 | async-start | bytes 2621440 | tf_op jit(solution)/shard_map/reduce_scatter | solution.py:257
  770.7 231.8 %reduce-scatter.33.cloned.1.call-start = ((), (), s32[]{:S(2)}) async-start(), calls=%async_computation.34 | async-start | bytes 540672
  796.8 320.2 %reduce-scatter.31.cloned.1.call-start = ((), (), s32[]{:S(2)}) async-start(), calls=%async_computation.33 | async-start | bytes 540672
  796.9 47.5 %copy-start.8 = (bf16[2,256,1024]{2,1,0:T(8,128)(2,1)S(1)}, bf16[2,256,1024]{2,1,0:T(8,128)(2,1)}, u32[]{:S(2)}) copy-start(bf16[2,256,1024]{2,1,0:T(8,128)(2,1)} %param.11) | copy-start | bytes 3145732
  796.9 47.5 %copy-start.39 = (bf16[16,64,256]{2,1,0:T(8,128)(2,1)S(1)}, bf16[16,64,256]{2,1,0:T(8,128)(2,1)}, u32[]{:S(2)}) copy-start(bf16[16,64,256]{2,1,0:T(8,128)(2,1)} %fusion.68) | copy-start | bytes 1572868
  796.9 47.5 %copy-start.45 = (f32[1024,1]{0,1:T(1,128)S(1)}, f32[1024,1]{0,1:T(1,128)}, u32[]{:S(2)}) copy-start(f32[1024,1]{0,1:T(1,128)} %copy-done.44) | copy-start | bytes 12292
  797.0 47.5 %copy-start.59 = (f32[256]{0:T(256)S(1)}, f32[256]{0:T(256)}, u32[]{:S(2)}) copy-start(f32[256]{0:T(256)} %copy-done.58) | copy-start | bytes 3076
  797.0 47.5 %copy-start.65 = (f32[256]{0:T(256)S(1)}, f32[256]{0:T(256)}, u32[]{:S(2)}) copy-start(f32[256]{0:T(256)} %copy-done.64) | copy-start | bytes 3076
  851.8 375.3 %reduce-scatter.29.cloned.1.call-start = ((), (), s32[]{:S(2)}) async-start(), calls=%async_computation.32 | async-start | bytes 6488064 | tf_op jit(solution)/shard_map/reduce_scatter | solution.py:297
  865.3 557.5 %reduce-scatter.27.cloned.1.call-start = ((), (), s32[]{:S(2)}) async-start(), calls=%async_computation.31 | async-start | bytes 12976128 | tf_op jit(solution)/shard_map/reduce_scatter | solution.py:294
  905.5 661.2 %reduce-scatter.25.cloned.1.call-start = ((), (), s32[]{:S(2)}) async-start(), calls=%async_computation.30 | async-start | bytes 4325376 | tf_op jit(solution)/shard_map/reduce_scatter | solution.py:286
  911.4 812.6 %reduce-scatter.23.cloned.1.call-start = ((), (), s32[]{:S(2)}) async-start(), calls=%async_computation.29 | async-start | bytes 12976128 | tf_op jit(solution)/shard_map/reduce_scatter | solution.py:285
  954.7 49.1 %copy-start.75 = (f32[256]{0:T(256)S(1)}, f32[256]{0:T(256)}, u32[]{:S(2)}) copy-start(f32[256]{0:T(256)} %copy-done.74) | copy-start | bytes 3076
  954.7 49.1 %copy-start.77 = (f32[256]{0:T(256)S(1)}, f32[256]{0:T(256)}, u32[]{:S(2)}) copy-start(f32[256]{0:T(256)} %copy-done.76) | copy-start | bytes 3076
  (50 other events, 325.4 us)
Sparse Core Ops, SparseCore 0:
  10.9 72.0 all-gather.9
  89.1 21.0 all-gather.11
  112.4 22.5 all-gather.13
  137.7 56.4 all-gather.15
  196.2 21.4 all-gather.21
  219.2 22.6 all-gather.19
  244.0 199.9 all-gather.17
  713.0 29.2 reduce-scatter.20
  745.4 31.1 reduce-scatter.18
  779.0 31.1 reduce-scatter.16
  813.3 31.1 reduce-scatter.14
  846.5 135.8 reduce-scatter.32
  985.2 131.7 reduce-scatter.30
  1120.5 106.5 reduce-scatter.28
  1230.5 192.1 reduce-scatter.26
  1425.4 141.2 reduce-scatter.24
  1573.2 150.7 reduce-scatter.22
